TPU v7x, 16 devices: a 4x2x1 block of a 4x4x8 slice. The times are simulated.
16 devices in a mesh: rep: 2 (over y, z), dp: 8 (over x, core).
Axes of the slice: x: 4, y: 2, z: 1, core: 2. Of those that a mesh axis runs over, the one named last changes fastest.
The devices are a block of a 4x4x8 slice.
Arguments:
- hidden: bfloat16 [512, 2048], P(('rep', 'dp')), parts along dimension 0
- lengths: int32 [512], P(('rep', 'dp')), parts along dimension 0
- kv_cache: bfloat16 [2, 512, 128, 576], P(None, ('rep', 'dp')), parts along dimension 1
- norm_attn: float32 [2, 2048], replicated
- w_q: bfloat16 [2, 2048, 9216], replicated
- w_o: bfloat16 [2, 8192, 2048], replicated
- norm_ffn: float32 [2, 2048], replicated
- w_gate: bfloat16 [2, 2048, 11264], P(None, None, 'dp')
- w_up: bfloat16 [2, 2048, 11264], P(None, None, 'dp')
- w_down: bfloat16 [2, 11264, 2048], P(None, 'dp')
- norm_final: float32 [2048], replicated
- w_head: bfloat16 [2048, 163840], P(None, 'dp')
Outputs:
- output: float32 [512, 163840], P('rep', 'dp'), parts along dimension 0
There are 2 independent parts. A program takes and returns all parts, laid end to end along the dimension named above; an argument that names none is the same for every part.
All inputs are finite; a program needn't handle non-finite values.
Results may differ from a plain program's by a relative error of at most 0.02.
Values are sent between devices in bfloat16 or wider.
A program may use at most 768 MiB of HBM per device.

v0:
```python
import jax
import jax.numpy as jnp
from jax import lax
from jax.sharding import PartitionSpec as P

LATENT_DIM = 512
QK_SCALE = 192 ** -0.5
NORM_EPS = 1e-6


def rms_norm(x_rows, gain_vec):
    x_float = x_rows.astype(jnp.float32)
    inv_rms = lax.rsqrt(jnp.mean(x_float * x_float, axis=-1, keepdims=True) + NORM_EPS)
    return (x_float * inv_rms * gain_vec).astype(jnp.bfloat16)


def mla_attention(normed, w_q, kv_cache, lengths):
    num_rows, seq_len, kv_width = kv_cache.shape
    q_heads = jnp.dot(normed, w_q, preferred_element_type=jnp.float32).astype(jnp.bfloat16)
    q_heads = q_heads.reshape(num_rows, -1, kv_width)
    scores = jnp.einsum('bhc,btc->bht', q_heads, kv_cache, preferred_element_type=jnp.float32) * QK_SCALE
    key_pos = lax.broadcasted_iota(jnp.int32, (1, 1, seq_len), 2)
    scores = jnp.where(key_pos < lengths[:, None, None], scores, -1e30)
    attn_probs = jax.nn.softmax(scores, axis=-1).astype(jnp.bfloat16)
    context = jnp.einsum('bht,btc->bhc', attn_probs, kv_cache[:, :, :LATENT_DIM], preferred_element_type=jnp.float32)
    return context.astype(jnp.bfloat16).reshape(num_rows, -1)


def ffn_block(normed, w_gate, w_up, w_down):
    gate_proj = jnp.dot(normed, w_gate, preferred_element_type=jnp.float32)
    up_proj = jnp.dot(normed, w_up, preferred_element_type=jnp.float32)
    act_rows = (jax.nn.silu(gate_proj) * up_proj).astype(jnp.bfloat16)
    return jnp.dot(act_rows, w_down, preferred_element_type=jnp.float32)


def add_residual(x_rows, delta):
    return (x_rows.astype(jnp.float32) + delta).astype(jnp.bfloat16)


def solution(mesh):
    row_axes = ('rep', 'dp')
    specs_in = (P(row_axes, None), P(row_axes), P(None, row_axes, None, None), P(), P(), P(), P(),
                P(None, None, 'dp'), P(None, None, 'dp'), P(None, 'dp', None), P(), P(None, 'dp'))

    def device_step(hidden, lengths, kv_cache, norm_attn, w_q, w_o, norm_ffn, w_gate, w_up, w_down, norm_final, w_head):
        x_rows = hidden
        for layer_idx in range(kv_cache.shape[0]):
            normed = rms_norm(x_rows, norm_attn[layer_idx])
            context = mla_attention(normed, w_q[layer_idx], kv_cache[layer_idx], lengths)
            x_rows = add_residual(x_rows, jnp.dot(context, w_o[layer_idx], preferred_element_type=jnp.float32))
            normed = rms_norm(x_rows, norm_ffn[layer_idx])
            gathered = lax.all_gather(normed, 'dp', axis=0, tiled=True)
            part_sum = ffn_block(gathered, w_gate[layer_idx], w_up[layer_idx], w_down[layer_idx])
            ffn_out = lax.psum_scatter(part_sum, 'dp', scatter_dimension=0, tiled=True)
            x_rows = add_residual(x_rows, ffn_out)
        normed = rms_norm(x_rows, norm_final)
        gathered = lax.all_gather(normed, 'dp', axis=0, tiled=True)
        return jnp.dot(gathered, w_head, preferred_element_type=jnp.float32)

    return jax.shard_map(device_step, mesh=mesh, in_specs=specs_in, out_specs=P('rep', 'dp'), check_vma=False)
```

profile of v0, /device:TPU:113, one launch (start us, length us, event | category | flops | bytes accessed | tf_op | source)
XLA Modules:
  0.0 286.5 jit_solution(2344031401492741996)
XLA Ops:
  6.6 1.0 fusion.91
  9.1 0.8 fusion.109
  10.0 15.2 %fusion.14 = bf16[32,9216]{1,0:T(8,128)(2,1)S(1)} fusion(bf16[2,2048,9216]{2,1,0:T(8,128)(2,1)} %param.16, bf16[32,2048]{1,0:T(8,128)(2,1)} %param.12, f32[2048]{0:T(1024)S(1)} %bitcast.99, f32[32]{0:T(128)S(1)} %add_rsqrt_fusion.4), kind=kOutput, calls=%fused_computation.14 | convolution fusion | flops 1208516608 | bytes 38477952 | tf_op jit(solution)/shard_map/dot_general | solution.py:19
  25.2 1.4 reshape.78
  26.6 8.3 %slice_bitcast_fusion.1 = (bf16[32,128,576]{1,2,0:T(8,128)(2,1)}, bf16[32,128,576]{1,2,0:T(8,128)(2,1)}) fusion(bf16[2,32,128,576]{2,3,1,0:T(8,128)(2,1)} %param.14), kind=kLoop, calls=%fused_computation.35 | loop fusion | bytes 18874368 | tf_op jit(solution)/shard_map/squeeze | solution.py:49
  34.9 1.9 fusion.81
  37.1 3.4 %fusion.72 = bf16[32,16,512]{2,1,0:T(8,128)(2,1)S(1)} fusion(bf16[32,128,576]{1,2,0:T(8,128)(2,1)} %get-tuple-element.9, f32[32,16]{1,0:T(8,128)S(1)} %fusion.111, f32[32,16,128]{2,1,0:T(8,128)S(1)} %fusion.81), kind=kOutput, calls=%fused_computation.50 | convolution fusion | flops 67568256 | bytes 5259264 | tf_op jit(solution)/shard_map/bht,btc->bhc/dot_general | solution.py:25
  40.9 13.7 %multiply_reduce_fusion.1 = (f32[32]{0:T(128)S(1)}, f32[32,2048]{1,0:T(8,128)S(1)}) fusion(bf16[32,8192]{1,0:T(8,128)(2,1)S(1)} %bitcast.94, bf16[2,8192,2048]{2,1,0:T(8,128)(2,1)} %param.17, bf16[32,2048]{1,0:T(8,128)(2,1)S(1)} %copy-done), kind=kOutput, calls=%fused_computation.81 | convolution fusion | flops 1074135040 | bytes 34472064 | tf_op jit(solution)/shard_map/dot_general | solution.py:50
  55.6 22.2 %all-gather.4.cloned.1.call-done = bf16[256,2048]{1,0:T(8,128)(2,1)} async-done(((bf16[32,2048]{1,0:T(8,128)(2,1)}), bf16[256,2048]{1,0:T(8,128)(2,1)}) %all-gather.4.cloned.1.call-update) | async-done | bytes 1048592 | tf_op jit(solution)/shard_map/all_gather | solution.py:52
  77.9 4.8 %fusion.30 = f32[256,1408]{1,0:T(8,128)S(1)} fusion(bf16[256,2048]{1,0:T(8,128)(2,1)} %all-gather.4.cloned.1.call-done, bf16[2,2048,1408]{2,1,0:T(8,128)(2,1)} %param.19), kind=kOutput, calls=%fused_computation.26 | convolution fusion | flops 1476395008 | bytes 8257536 | tf_op jit(solution)/shard_map/dot_general | solution.py:30
  82.7 9.1 %fusion.26 = f32[256,2048]{1,0:T(8,128)} fusion(bf16[2,1408,2048]{2,1,0:T(8,128)(2,1)} %param.21, bf16[256,2048]{1,0:T(8,128)(2,1)S(1)} %copy-done.2, bf16[2,2048,1408]{2,1,0:T(8,128)(2,1)} %param.20, f32[256,1408]{1,0:T(8,128)S(1)} %fusion.30), kind=kOutput, calls=%fused_computation.22 | convolution fusion | flops 2954952704 | bytes 16121856 | tf_op jit(solution)/shard_map/dot_general | solution.py:33
  92.0 26.2 %reduce-scatter.3.cloned.1.call-done = f32[32,2048]{1,0:T(8,128)} async-done(((f32[256,2048]{1,0:T(8,128)}), f32[32,2048]{1,0:T(8,128)}) %reduce-scatter.3.cloned.1.call-update) | async-done | bytes 262160 | tf_op jit(solution)/shard_map/reduce_scatter | solution.py:54
  118.2 1.1 fusion.94
  119.3 15.2 %fusion.17 = bf16[32,9216]{1,0:T(8,128)(2,1)S(1)} fusion(bf16[2,2048,9216]{2,1,0:T(8,128)(2,1)} %param.16, bf16[32,2048]{1,0:T(8,128)(2,1)S(1)} %get-tuple-element.8, f32[2048]{0:T(1024)S(1)} %bitcast.98, f32[32]{0:T(128)S(1)} %add_rsqrt_fusion.2), kind=kOutput, calls=%fused_computation.15 | convolution fusion | flops 1208516608 | bytes 38477952 | tf_op jit(solution)/shard_map/dot_general | solution.py:19
  135.0 3.1 %fusion.80 = f32[32,16,128]{2,1,0:T(8,128)S(1)} fusion(bf16[32,16,576]{2,1,0:T(8,128)(2,1)S(1)} %reshape.80, pred[32,128]{1,0:T(8,128)(4,1)S(1)} %iota_compare_fusion, bf16[2,32,128,576]{2,3,1,0:T(8,128)(2,1)} %param.14), kind=kOutput, calls=%fused_computation.55 | convolution fusion | flops 75628544 | bytes 5574656 | tf_op jit(solution)/shard_map/bhc,btc->bht/dot_general | solution.py:21
  138.4 3.4 %fusion.75 = bf16[32,16,512]{2,1,0:T(8,128)(2,1)S(1)} fusion(bf16[32,128,576]{1,2,0:T(8,128)(2,1)} %get-tuple-element.10, f32[32,16]{1,0:T(8,128)S(1)} %fusion.112, f32[32,16,128]{2,1,0:T(8,128)S(1)} %fusion.80), kind=kOutput, calls=%fused_computation.51 | convolution fusion | flops 67568256 | bytes 5259264 | tf_op jit(solution)/shard_map/bht,btc->bhc/dot_general | solution.py:25
  142.2 13.7 %multiply_reduce_fusion = (f32[32]{0:T(128)S(1)}, f32[32,2048]{1,0:T(8,128)S(1)}) fusion(bf16[32,8192]{1,0:T(8,128)(2,1)S(1)} %bitcast.92, bf16[2,8192,2048]{2,1,0:T(8,128)(2,1)} %param.17, bf16[32,2048]{1,0:T(8,128)(2,1)S(1)} %get-tuple-element.8), kind=kOutput, calls=%fused_computation.77 | convolution fusion | flops 1074135040 | bytes 34472064 | tf_op jit(solution)/shard_map/dot_general | solution.py:50
  157.0 21.2 %all-gather.6.cloned.1.call-done = bf16[256,2048]{1,0:T(8,128)(2,1)} async-done(((bf16[32,2048]{1,0:T(8,128)(2,1)}), bf16[256,2048]{1,0:T(8,128)(2,1)}) %all-gather.6.cloned.1.call-update) | async-done | bytes 1048592 | tf_op jit(solution)/shard_map/all_gather | solution.py:52
  178.2 4.8 %fusion.24 = f32[256,1408]{1,0:T(8,128)S(1)} fusion(bf16[256,2048]{1,0:T(8,128)(2,1)} %all-gather.6.cloned.1.call-done, bf16[2,2048,1408]{2,1,0:T(8,128)(2,1)} %param.19), kind=kOutput, calls=%fused_computation.20 | convolution fusion | flops 1476395008 | bytes 8257536 | tf_op jit(solution)/shard_map/dot_general | solution.py:30
  183.1 9.2 %fusion.20 = f32[256,2048]{1,0:T(8,128)} fusion(bf16[2,1408,2048]{2,1,0:T(8,128)(2,1)} %param.21, bf16[256,2048]{1,0:T(8,128)(2,1)S(1)} %copy-done.3, bf16[2,2048,1408]{2,1,0:T(8,128)(2,1)} %param.20, f32[256,1408]{1,0:T(8,128)S(1)} %fusion.24), kind=kOutput, calls=%fused_computation.16 | convolution fusion | flops 2954952704 | bytes 16121856 | tf_op jit(solution)/shard_map/dot_general | solution.py:33
  192.5 26.3 %reduce-scatter.5.cloned.1.call-done = f32[32,2048]{1,0:T(8,128)} async-done(((f32[256,2048]{1,0:T(8,128)}), f32[32,2048]{1,0:T(8,128)}) %reduce-scatter.5.cloned.1.call-update) | async-done | bytes 262160 | tf_op jit(solution)/shard_map/reduce_scatter | solution.py:54
  218.7 1.1 fusion.88
  220.6 21.4 %all-gather.8.cloned.1.call-done = bf16[256,2048]{1,0:T(8,128)(2,1)} async-done(((bf16[32,2048]{1,0:T(8,128)(2,1)}), bf16[256,2048]{1,0:T(8,128)(2,1)}) %all-gather.8.cloned.1.call-update) | async-done | bytes 1048592 | tf_op jit(solution)/shard_map/all_gather | solution.py:57
  242.0 38.0 %fusion.113 = f32[256,20480]{1,0:T(8,128)} fusion(bf16[256,2048]{1,0:T(8,128)(2,1)} %all-gather.8.cloned.1.call-done, bf16[2048,20480]{1,0:T(8,128)(2,1)} %param.23), kind=kOutput, calls=%fused_computation.103 | convolution fusion | flops 21474836480 | bytes 105906176 | tf_op jit(solution)/shard_map/dot_general | solution.py:58
  (40 shorter events, 6.5 us)
Async XLA Ops:
  6.5 71.3 %all-gather.4.cloned.1.call-start = ((), (), s32[]{:S(2)}) async-start(), calls=%async_computation.2 | async-start | bytes 1179648 | tf_op jit(solution)/shard_map/all_gather | solution.py:52
  25.2 9.7 %slice-start = ((s8[9437184]{0:T(1024)(128)(4,1)}), s8[1048576]{0:T(1024)(128)(4,1)S(1)}, s32[]{:S(2)}) async-start(s8[9437184]{0:T(1024)(128)(4,1)} %bitcast.90), calls=%async_computation.7 | async-start | bytes 2097152
  26.5 8.3 %slice-start.1 = ((s8[9437184]{0:T(1024)(128)(4,1)}), s8[4194304]{0:T(1024)(128)(4,1)S(1)}, s32[]{:S(2)}) async-start(s8[9437184]{0:T(1024)(128)(4,1)} %bitcast.90), calls=%async_computation.8 | async-start | bytes 8388608
  26.6 8.3 %slice-start.2 = ((s8[9437184]{0:T(1024)(128)(4,1)}), s8[4194304]{0:T(1024)(128)(4,1)S(1)}, s32[]{:S(2)}) async-start(s8[9437184]{0:T(1024)(128)(4,1)} %bitcast.90), calls=%async_computation.9 | async-start | bytes 8388608
  34.9 5.9 %copy-start = (bf16[32,2048]{1,0:T(8,128)(2,1)S(1)}, bf16[32,2048]{1,0:T(8,128)(2,1)}, u32[]{:S(2)}) copy-start(bf16[32,2048]{1,0:T(8,128)(2,1)} %param.12) | copy-start | bytes 393220
  55.4 62.8 %reduce-scatter.3.cloned.1.call-start = ((), (), s32[]{:S(2)}) async-start(), calls=%async_computation.3 | async-start | bytes 2359296 | tf_op jit(solution)/shard_map/reduce_scatter | solution.py:54
  77.9 4.8 %copy-start.2 = (bf16[256,2048]{1,0:T(8,128)(2,1)S(1)}, bf16[256,2048]{1,0:T(8,128)(2,1)}, u32[]{:S(2)}) copy-start(bf16[256,2048]{1,0:T(8,128)(2,1)} %all-gather.4.cloned.1.call-done) | copy-start | bytes 3145732
  91.9 86.3 %all-gather.6.cloned.1.call-start = ((), (), s32[]{:S(2)}) async-start(), calls=%async_computation.4 | async-start | bytes 1179648 | tf_op jit(solution)/shard_map/all_gather | solution.py:52
  156.7 62.0 %reduce-scatter.5.cloned.1.call-start = ((), (), s32[]{:S(2)}) async-start(), calls=%async_computation.5 | async-start | bytes 2359296 | tf_op jit(solution)/shard_map/reduce_scatter | solution.py:54
  178.2 4.8 %copy-start.3 = (bf16[256,2048]{1,0:T(8,128)(2,1)S(1)}, bf16[256,2048]{1,0:T(8,128)(2,1)}, u32[]{:S(2)}) copy-start(bf16[256,2048]{1,0:T(8,128)(2,1)} %all-gather.6.cloned.1.call-done) | copy-start | bytes 3145732
  183.1 36.7 %copy-start.1 = (f32[2048]{0:T(1024)S(1)}, f32[2048]{0:T(1024)}, u32[]{:S(2)}) copy-start(f32[2048]{0:T(1024)} %param.22) | copy-start | bytes 24580
  192.4 49.6 %all-gather.8.cloned.1.call-start = ((), (), s32[]{:S(2)}) async-start(), calls=%async_computation.6 | async-start | bytes 1179648 | tf_op jit(solution)/shard_map/all_gather | solution.py:57
Sparse Core Ops, SparseCore 0:
  55.5 22.2 all-gather.3
  92.0 26.1 reduce-scatter.2
  156.8 21.3 all-gather.5
  192.5 26.1 reduce-scatter.4
  220.8 21.2 all-gather.7
where the time goes:
time: 287 us
  matrix products  136 us (47%)
  waiting for transfers between devices  118 us (41%)
  between operations  13.3 us (5%)
  local copies, waits for them, and re-layouts  12.5 us (4%)
  other arithmetic  6.73 us (2%)
    all_gather x3, waiting for transfers between devices, device_step(): gathered = lax.all_gather(normed, 'dp', axis=0, tiled=True)  64.8 us
    reduce_scatter x2, waiting for transfers between devices, device_step(): ffn_out = lax.psum_scatter(part_sum, 'dp', scatter_dimension=0, tiled=True)  52.4 us
    dot_general x1, matrix products, device_step(): return jnp.dot(gathered, w_head, preferred_element_type=jnp.float32)  38 us
    dot_general x2, matrix products, mla_attention(): jnp.dot(normed, w_q, preferred_element_type=jnp.float32)  30.4 us
    dot_general x2, matrix products, device_step(): jnp.dot(context, w_o[layer_idx], preferred_element_type=jnp.float32)  27.4 us
    dot_general x2, matrix products, ffn_block(): return jnp.dot(act_rows, w_down, preferred_element_type=jnp.float32)  18.4 us
    dot_general x2, matrix products, ffn_block(): gate_proj = jnp.dot(normed, w_gate, preferred_element_type=jnp.float32)  9.66 us
    squeeze x1, local copies, waits for them, and re-layouts, device_step(): kv_cache[layer_idx]  8.34 us
  transfers between devices with their start and end apart: 5, of which 5 were waited for; matrix products, arithmetic and copies ran while one was open for 0% of the time, Pallas kernels for 0%

commit v1 on v0

v1 whole, which is shorter than its diff:
```python
import functools

import jax
import jax.numpy as jnp
from jax import lax
from jax.experimental import pallas as pl
from jax.experimental.pallas import tpu as pltpu
from jax.sharding import PartitionSpec as P

LATENT_DIM = 512
QK_SCALE = 192 ** -0.5
NORM_EPS = 1e-6
MESH = pl.DeviceIdType.MESH
BF16, F32 = jnp.bfloat16, jnp.float32
TILE = 256
LANES = 128
GROUP = 8


def rms_norm(x_float, gain_row):
    inv_rms = lax.rsqrt(jnp.mean(x_float * x_float, axis=-1, keepdims=True) + NORM_EPS)
    return (x_float * inv_rms * gain_row).astype(BF16)


def decode_kernel(cfg, lengths, hidden, kv_hbm, norm_attn, wq_hbm, wo_hbm, norm_ffn, wg_hbm, wu_hbm, wd_hbm, norm_final,
                  out, wa, wb, kv_b, x_full, h_s, q_s, o_s, o_all, xg, act, y_send, y_recv, y_sum, relay_in, relay_out,
                  direct_in, w_sem, kv_sem, x_send, x_recv, q_send, q_recv, o_send, o_recv, ag_send, ag_recv,
                  d2d_send, d2d_recv, y_ssem, y_rsem, rs_send, rs_recv):
    num_layers, rows, heads, width, d_model, ffn, n_dev = cfg
    chips = n_dev // 2
    pair = 2 * rows
    half_d = d_model // 2
    half_h = heads // 2
    q_cols = half_h * width
    t_tiles = half_d // TILE
    q_parts = q_s.shape[0]

    me = lax.axis_index("dp")
    chip, core = lax.div(me, 2), lax.rem(me, 2)
    other = 1 - core
    partner = chip * 2 + other
    right_chip, left_chip = lax.rem(chip + 1, chips), lax.rem(chip + chips - 1, chips)
    far_chip = lax.rem(chip + 2, chips)
    right, left = right_chip * 2 + core, left_chip * 2 + core

    def remote(src, dst, send_sem, recv_sem, device):
        return pltpu.make_async_remote_copy(src_ref=src, dst_ref=dst, send_sem=send_sem, recv_sem=recv_sem,
                                            device_id={"dp": device}, device_id_type=MESH)

    pair_cols = 2 * width
    n_q = q_cols // pair_cols
    n_o = 4
    o_depth = wo_hbm.shape[1] // n_o
    kv_parts = rows // GROUP

    def q_copy(l, p):
        col = pl.multiple_of(core * q_cols + p * pair_cols, LANES)
        return pltpu.make_async_copy(wq_hbm.at[l, :, pl.ds(col, pair_cols)],
                                     wa.at[:, p * pair_cols:(p + 1) * pair_cols], w_sem.at[p])

    def o_copy(l, p):
        col = pl.multiple_of(core * half_d, LANES)
        return pltpu.make_async_copy(wo_hbm.at[l, p * o_depth:(p + 1) * o_depth, pl.ds(col, half_d)],
                                     wb.at[p * o_depth:(p + 1) * o_depth, :], w_sem.at[n_q + p])

    def ffn_copies(l):
        return [pltpu.make_async_copy(wg_hbm.at[l], wa.at[:, 0:ffn], w_sem.at[n_q + n_o]),
                pltpu.make_async_copy(wu_hbm.at[l], wa.at[:, ffn:2 * ffn], w_sem.at[n_q + n_o + 1]),
                pltpu.make_async_copy(wd_hbm.at[l], wa.at[0:ffn, 2 * ffn:2 * ffn + d_model], w_sem.at[n_q + n_o + 2])]

    def kv_copy(l, g):
        return pltpu.make_async_copy(kv_hbm.at[l, g * GROUP:(g + 1) * GROUP],
                                     kv_b.at[g * GROUP:(g + 1) * GROUP], kv_sem.at[g])

    for p in range(n_q):
        q_copy(0, p).start()
    for g in range(kv_parts):
        kv_copy(0, g).start()
    for p in range(n_o):
        o_copy(0, p).start()

    barrier = pltpu.get_barrier_semaphore()
    for device in (partner, left, right):
        pl.semaphore_signal(barrier, inc=1, device_id={"dp": device}, device_id_type=MESH)
    pl.semaphore_wait(barrier, 3)

    if width % LANES:
        q_s[q_parts - 1] = jnp.zeros(q_s.shape[1:], F32)

    own_rows = pl.ds(pl.multiple_of(core * rows, rows), rows)
    first = remote(hidden, x_full.at[own_rows, :], x_send.at[0], x_recv.at[0], partner)
    first.start()
    x_full[own_rows, :] = hidden[...]
    first.wait()

    def half_cols(which, t=0, n=None):
        return pl.ds(pl.multiple_of(which * half_d + t * TILE, LANES), half_d if n is None else n)

    def gather_rows(gain_row, dst):
        def piece(which_chip, half, count=rows):
            return xg.at[pl.ds(pl.multiple_of(which_chip * pair + half * rows, rows), count), half_cols(core)]

        def send(which_chip, half, slot, device):
            copy = remote(piece(which_chip, half), piece(which_chip, half), ag_send.at[slot], ag_recv.at[slot], device)
            copy.start()
            return copy

        def pass_on(which_chip, half, slot, count=rows):
            copy = remote(piece(which_chip, half, count), piece(which_chip, half, count),
                          d2d_send.at[slot], d2d_recv.at[slot], partner)
            copy.start()
            return copy

        def norm(which_chip):
            at = pl.ds(pl.multiple_of(which_chip * pair, pair), pair)
            dst[at, :] = rms_norm(xg[at, :].astype(F32), gain_row)

        own_a = send(chip, 0, 0, right)
        own_b = send(chip, 1, 1, left)
        own_b2 = send(chip, 1, 2, right)
        own_a2 = send(chip, 0, 3, left)
        passed = [pass_on(chip, 0, 0, pair)]
        own_a.wait_recv()
        far_a = send(left_chip, 0, 4, right)
        own_b.wait_recv()
        far_b = send(right_chip, 1, 5, left)
        passed.append(pass_on(left_chip, 0, 1))
        passed.append(pass_on(right_chip, 1, 2))
        passed[0].wait_recv()
        norm(chip)
        own_b2.wait_recv()
        passed.append(pass_on(left_chip, 1, 3))
        own_a2.wait_recv()
        passed.append(pass_on(right_chip, 0, 4))
        passed[1].wait_recv()
        passed[3].wait_recv()
        norm(left_chip)
        passed[2].wait_recv()
        passed[4].wait_recv()
        norm(right_chip)
        far_a.wait_recv()
        passed.append(pass_on(far_chip, 0, 5))
        far_b.wait_recv()
        passed.append(pass_on(far_chip, 1, 6))
        passed[5].wait_recv()
        passed[6].wait_recv()
        norm(far_chip)
        for copy in [own_a, own_b, own_b2, own_a2, far_a, far_b] + passed:
            copy.wait_send()

    own_chip_rows = pl.ds(pl.multiple_of(chip * pair, pair), pair)

    for layer in range(num_layers):
        h_s[...] = rms_norm(x_full[...].astype(F32), norm_attn[layer:layer + 1, :])
        q_copies = []
        for p in range(n_q):
            q_copy(layer, p).wait()
            q_val = jnp.dot(h_s[...], wa[:, p * pair_cols:(p + 1) * pair_cols], preferred_element_type=F32)
            q_val = q_val.astype(BF16).astype(F32)
            for e in range(2):
                head = core * half_h + 2 * p + e
                base = pl.multiple_of(head * pair, pair)
                q_head = q_val[:, e * width:(e + 1) * width]
                for c in range(q_parts):
                    lanes = min(LANES, width - c * LANES)
                    q_s[c, pl.ds(base, pair), 0:lanes] = q_head[:, c * LANES:c * LANES + lanes]
                away = pl.ds(pl.multiple_of(base + other * rows, rows), rows)
                copy = remote(q_s.at[:, away, :], q_s.at[:, away, :], q_send.at[2 * p + e], q_recv.at[2 * p + e], partner)
                copy.start()
                q_copies.append(copy)
        for copy in ffn_copies(layer):
            copy.start()
        for copy in q_copies:
            copy.wait_recv()

        o_copies = []
        per_half = kv_parts // 2
        key_pos = lax.broadcasted_iota(jnp.int32, (heads, kv_b.shape[1]), 1)
        for half in range(2):
            for g in range(half * per_half, (half + 1) * per_half):
                kv_copy(layer, g).wait()
                scores = []
                for i in range(GROUP):
                    b = g * GROUP + i
                    at = pl.ds(core * rows + b, heads, stride=pair)
                    q_b = jnp.concatenate([q_s[c, at, :] for c in range(q_parts)], axis=1)[:, 0:width].astype(BF16)
                    s_b = lax.dot_general(q_b, kv_b[b], (((1,), (1,)), ((), ())), preferred_element_type=F32) * QK_SCALE
                    scores.append(jnp.where(key_pos < lengths[b], s_b, -1e30))
                s_all = jnp.concatenate(scores, axis=0)
                e_all = jnp.exp(s_all - jnp.max(s_all, axis=-1, keepdims=True))
                p_all = (e_all / jnp.sum(e_all, axis=-1, keepdims=True)).astype(BF16)
                for i in range(GROUP):
                    b = g * GROUP + i
                    o_b = jnp.dot(p_all[i * heads:(i + 1) * heads, :], kv_b[b, :, 0:LATENT_DIM], preferred_element_type=F32)
                    for c in range(LATENT_DIM // LANES):
                        o_s[c, pl.ds(b, heads, stride=rows), :] = o_b[:, c * LANES:(c + 1) * LANES]
                if layer + 1 < num_layers:
                    kv_copy(layer + 1, g).start()
            part = rows // 2
            at = pl.ds(pl.multiple_of(core * rows + half * part, part), part)
            for head in range(heads):
                for c in range(LATENT_DIM // LANES):
                    o_all[at, head * LATENT_DIM + c * LANES:head * LATENT_DIM + (c + 1) * LANES] = \
                        o_s[c, head * rows + half * part:head * rows + (half + 1) * part, :].astype(BF16)
            copy = remote(o_all.at[at, :], o_all.at[at, :], o_send.at[half], o_recv.at[half], partner)
            copy.start()
            o_copies.append(copy)
        for copy in q_copies:
            copy.wait_send()

        for p in range(n_o):
            o_copy(layer, p).wait()
        for copy in o_copies:
            copy.wait_recv()

        def wo_tile(t, carry):
            cols = pl.ds(pl.multiple_of(t * TILE, TILE), TILE)
            o_val = jnp.dot(o_all[...], wb[:, cols], preferred_element_type=F32)
            xg[own_chip_rows, half_cols(core, t, TILE)] = \
                (x_full[:, half_cols(core, t, TILE)].astype(F32) + o_val).astype(BF16)
            return carry

        lax.fori_loop(0, t_tiles, wo_tile, 0)
        for copy in o_copies:
            copy.wait_send()
        if layer + 1 < num_layers:
            for p in range(n_o):
                o_copy(layer + 1, p).start()

        gather_rows(norm_ffn[layer:layer + 1, :], out)
        for copy in ffn_copies(layer):
            copy.wait()

        def gate_up(j, carry):
            at = pl.ds(pl.multiple_of(j * LANES, LANES), LANES)
            at_up = pl.ds(pl.multiple_of(ffn + j * LANES, LANES), LANES)
            both = jnp.concatenate([wa[:, at], wa[:, at_up]], axis=1)
            val = jnp.dot(out[...], both, preferred_element_type=F32)
            act[:, at] = (jax.nn.silu(val[:, :LANES]) * val[:, LANES:]).astype(BF16)
            return carry

        lax.fori_loop(0, ffn // LANES, gate_up, 0)

        def down(which, t):
            cols = pl.ds(pl.multiple_of(2 * ffn + which * half_d + t * TILE, LANES), TILE)
            return jnp.dot(act[...], wa[0:ffn, cols], preferred_element_type=F32)

        y_copies = []
        for t in range(t_tiles):
            y_send[t] = down(other, t)
            copy = remote(y_send.at[t], y_recv.at[t], y_ssem.at[t], y_rsem.at[t], partner)
            copy.start()
            y_copies.append(copy)

        def rows_of(which_chip, half):
            return pl.ds(pl.multiple_of(which_chip * pair + half * rows, rows), rows)

        def rs_copy(src, dst, slot, t, device):
            copy = remote(src, dst, rs_send.at[slot, t], rs_recv.at[slot, t], device)
            copy.start()
            return copy

        rs_relay, rs_direct, rs_final = [], [], []

        def relay(t):
            for d, device, target in ((0, right, right_chip), (1, left, left_chip)):
                rs_relay[t][d].wait_recv()
                relay_out[d, t] = relay_in[d, t] + y_sum[t, rows_of(target, d), :]
                rs_final[t].append(rs_copy(relay_out.at[d, t], direct_in.at[2 + d, t], 4 + d, t, device))

        for t in range(t_tiles):
            own = down(core, t)
            y_copies[t].wait_recv()
            y_sum[t] = own + y_recv[t]
            rs_relay.append([rs_copy(y_sum.at[t, rows_of(far_chip, 0), :], relay_in.at[0, t], 0, t, right),
                             rs_copy(y_sum.at[t, rows_of(far_chip, 1), :], relay_in.at[1, t], 1, t, left)])
            rs_direct.append([rs_copy(y_sum.at[t, rows_of(right_chip, 1), :], direct_in.at[0, t], 2, t, right),
                              rs_copy(y_sum.at[t, rows_of(left_chip, 0), :], direct_in.at[1, t], 3, t, left)])
            rs_final.append([])
            if t >= 1:
                relay(t - 1)
        relay(t_tiles - 1)
        if layer + 1 < num_layers:
            for p in range(n_q):
                q_copy(layer + 1, p).start()

        last = layer + 1 == num_layers
        x_copies = []
        for t in range(t_tiles):
            for copy in rs_direct[t] + rs_final[t]:
                copy.wait_recv()
            cols = half_cols(core, t, TILE)
            for half in range(2):
                total = (y_sum[t, rows_of(chip, half), :] + direct_in[2 + half, t]) + direct_in[1 - half, t]
                x_new = (xg[rows_of(chip, half), cols].astype(F32) + total).astype(BF16)
                if last:
                    xg[rows_of(chip, half), cols] = x_new
                else:
                    x_full[half * rows:(half + 1) * rows, cols] = x_new
            if not last:
                copy = remote(x_full.at[:, cols], x_full.at[:, cols], x_send.at[1 + t], x_recv.at[1 + t], partner)
                copy.start()
                x_copies.append(copy)
        for copy in y_copies:
            copy.wait_send()
        for group in rs_relay + rs_direct + rs_final:
            for copy in group:
                copy.wait_send()
        for copy in x_copies:
            copy.wait()

    gather_rows(norm_final[0:1, :], out)


def decode_layers(n_dev, lengths, hidden, kv_cache, norm_attn, w_q, w_o, norm_ffn, w_gate, w_up, w_down, norm_final):
    num_layers, rows, seq_len, width = kv_cache.shape
    d_model = hidden.shape[1]
    heads = w_q.shape[2] // width
    ffn = w_gate.shape[2]
    pair, group_rows, half_d = 2 * rows, n_dev * rows, d_model // 2
    q_cols = heads * width // 2
    wa_cols = max(q_cols, 2 * ffn + d_model)
    wa_cols = -(-wa_cols // LANES) * LANES
    t_tiles = half_d // TILE
    pad_width = -(-width // LANES) * LANES
    hbm, vmem = pl.BlockSpec(memory_space=pl.ANY), pl.BlockSpec(memory_space=pltpu.VMEM)
    smem = pl.BlockSpec(memory_space=pltpu.SMEM)
    dma = pltpu.SemaphoreType.DMA
    cfg = (num_layers, rows, heads, width, d_model, ffn, n_dev)
    n_q = q_cols // (2 * width)
    scratch = [
        pltpu.VMEM((d_model, wa_cols), BF16),
        pltpu.VMEM((w_o.shape[1], half_d), BF16),
        pltpu.VMEM((rows, seq_len, width), BF16),
        pltpu.VMEM((pair, d_model), BF16),
        pltpu.VMEM((pair, d_model), BF16),
        pltpu.VMEM((pad_width // LANES, heads * pair, LANES), F32),
        pltpu.VMEM((LATENT_DIM // LANES, heads * rows, LANES), F32),
        pltpu.VMEM((pair, heads * LATENT_DIM), BF16),
        pltpu.VMEM((group_rows, d_model), BF16),
        pltpu.VMEM((group_rows, ffn), BF16),
        pltpu.VMEM((t_tiles, group_rows, TILE), F32),
        pltpu.VMEM((t_tiles, group_rows, TILE), F32),
        pltpu.VMEM((t_tiles, group_rows, TILE), F32),
        pltpu.VMEM((2, t_tiles, rows, TILE), F32),
        pltpu.VMEM((2, t_tiles, rows, TILE), F32),
        pltpu.VMEM((4, t_tiles, rows, TILE), F32),
        dma((n_q + 4 + 3,)),
        dma((rows // GROUP,)),
        dma((1 + t_tiles,)), dma((1 + t_tiles,)),
        dma((2 * n_q,)), dma((2 * n_q,)),
        dma((2,)), dma((2,)),
        dma((6,)), dma((6,)),
        dma((7,)), dma((7,)),
        dma((t_tiles,)), dma((t_tiles,)),
        dma((6, t_tiles)), dma((6, t_tiles)),
    ]
    return pl.pallas_call(
        functools.partial(decode_kernel, cfg),
        out_shape=jax.ShapeDtypeStruct((group_rows, d_model), BF16),
        in_specs=[smem, vmem, hbm, vmem, hbm, hbm, vmem, hbm, hbm, hbm, vmem],
        out_specs=vmem,
        scratch_shapes=scratch,
        compiler_params=pltpu.CompilerParams(collective_id=0, has_side_effects=True, vmem_limit_bytes=64 * 1000 * 1000),
        name="decode_layers",
    )(lengths, hidden, kv_cache, norm_attn, w_q, w_o, norm_ffn, w_gate, w_up, w_down, norm_final.reshape(1, -1))


def solution(mesh):
    row_axes = ('rep', 'dp')
    specs_in = (P(row_axes, None), P(row_axes), P(None, row_axes, None, None), P(), P(), P(), P(),
                P(None, None, 'dp'), P(None, None, 'dp'), P(None, 'dp', None), P(), P(None, 'dp'))
    n_dev = mesh.shape['dp']

    def device_step(hidden, lengths, kv_cache, norm_attn, w_q, w_o, norm_ffn, w_gate, w_up, w_down, norm_final, w_head):
        gathered = decode_layers(n_dev, lengths, hidden, kv_cache, norm_attn, w_q, w_o, norm_ffn, w_gate, w_up, w_down,
                                 norm_final)
        return jnp.dot(gathered, w_head, preferred_element_type=jnp.float32)

    return jax.shard_map(device_step, mesh=mesh, in_specs=specs_in, out_specs=P('rep', 'dp'), check_vma=False)
```

time: 287 us -> 160 us (0.56)
  waiting for transfers between devices: 118 us -> 0 us
  Pallas kernels: 0 us -> 108 us
  matrix products: 136 us -> 38 us
  between operations: 13.3 us -> 0.01 us
  other arithmetic: 6.73 us -> 0 us
    pallas_call x0 -> x1, Pallas kernels: none -> 108 us  [decode_layers(): pl.pallas_call(functools.partial(decode_kernel, cfg), out_shape=jax.Shape...]
    dot_general x12 -> x0, matrix products: 97.8 us -> none  [the longest x2 30.4 us: mla_attention(): jnp.dot(normed, w_q, preferred_element_type=jnp.float32)]
    all_gather x3 -> x0, waiting for transfers between devices: 64.8 us -> none  [device_step(): gathered = lax.all_gather(normed, 'dp', axis=0, tiled=True)]
    reduce_scatter x2 -> x0, waiting for transfers between devices: 52.4 us -> none  [device_step(): ffn_out = lax.psum_scatter(part_sum, 'dp', scatter_dimension=0, tiled=True)]
    unnamed x16 -> x1, local copies, waits for them, and re-layouts: 0.68 us -> 13.6 us
    squeeze x1 -> x0, local copies, waits for them, and re-layouts: 8.34 us -> none  [device_step(): kv_cache[layer_idx]]
    reduce_sum x3 -> x0, other arithmetic: 3.22 us -> none  [rms_norm(): jnp.mean(x_float * x_float, axis=-1, keepdims=True) + NORM_EPS]
  transfers between devices with their start and end apart: 5 -> 0, of which waited for: 5 -> 0; matrix products, arithmetic and copies ran while one was open for 0% -> 0% of each run, Pallas kernels for 0% -> 0%
where the time goes in v1:
time: 160 us
  Pallas kernels  108 us (68%)
  matrix products  38 us (24%)
  local copies, waits for them, and re-layouts  13.6 us (8%)
    pallas_call x1, Pallas kernels, decode_layers(): pl.pallas_call(functools.partial(decode_kernel, cfg), out_shape=jax.Shape...  108 us
    dot_general x1, matrix products, device_step(): return jnp.dot(gathered, w_head, preferred_element_type=jnp.float32)  38 us
    unnamed x1, local copies, waits for them, and re-layouts  13.6 us

profile of v1, /device:TPU:113, one launch (start us, length us, event | category | flops | bytes accessed | tf_op | source)
XLA Modules:
  0.0 159.6 jit_solution(2645127811344002751)
XLA Ops:
  0.0 13.6 %copy.13.kv_hbm = bf16[2,32,128,576]{3,2,1,0:T(8,128)(2,1)} copy(bf16[2,32,128,576]{2,3,1,0:T(8,128)(2,1)} %param.14) | data formatting | bytes 18874368 | tf_op args[2]
  13.6 108.1 %decode_layers.1 = bf16[256,2048]{1,0:T(8,128)(2,1)} custom-call(s32[32]{0:T(128)} %lengths.1, bf16[32,2048]{1,0:T(8,128)(2,1)} %hidden.1, bf16[2,32,128,576]{3,2,1,0:T(8,128)(2,1)} %copy.13.kv_hbm, f32[2,2048]{1,0:T(2,128)} %norm_attn.1, bf16[2,2048,9216]{2,1,0:T(8,128)(2,1)} %wq_hbm.1, bf16[2,8192,2048]{2,1,0:T(8,128)(2,1)} %wo_hbm.1, f32[2,2048]{1,0:T(2,128)} %norm_ffn.1, ...), custom_call_target="tpu_custom_call" | custom-call | tf_op jit(solution)/shard_map/decode_layers/pallas_call | solution.py:358
  121.6 38.0 %fusion = f32[256,20480]{1,0:T(8,128)} fusion(bf16[256,2048]{1,0:T(8,128)(2,1)} %decode_layers.1, bf16[2048,20480]{1,0:T(8,128)(2,1)} %param.23), kind=kOutput, calls=%fused_computation | convolution fusion | flops 21474836480 | bytes 105906176 | tf_op jit(solution)/shard_map/dot_general | solution.py:378

commit v2 on v1

--- a/solution.py
+++ b/solution.py
@@ -14,6 +14,9 @@
 BF16, F32 = jnp.bfloat16, jnp.float32
 TILE = 256
 LANES = 128
+AG_LAG = 2
+AG_STRAIGHT = 2
+RS_LAG = 2
 GROUP = 8
 
 
@@ -23,8 +26,8 @@
 
 
 def decode_kernel(cfg, lengths, hidden, kv_hbm, norm_attn, wq_hbm, wo_hbm, norm_ffn, wg_hbm, wu_hbm, wd_hbm, norm_final,
-                  out, wa, wb, kv_b, x_full, h_s, q_s, o_s, o_all, xg, act, y_send, y_recv, y_sum, relay_in, relay_out,
-                  direct_in, w_sem, kv_sem, x_send, x_recv, q_send, q_recv, o_send, o_recv, ag_send, ag_recv,
+                  w_head_hbm, out, wa, kv_b, x_full, h_s, q_s, o_s, o_all, xg, act, y_send, y_recv, y_sum, relay_in, relay_out,
+                  direct_in, w_sem, kv_sem, head_sem, x_send, x_recv, q_send, q_recv, o_send, o_recv, ag_send, ag_recv,
                   d2d_send, d2d_recv, y_ssem, y_rsem, rs_send, rs_recv):
     num_layers, rows, heads, width, d_model, ffn, n_dev = cfg
     chips = n_dev // 2
@@ -41,7 +44,7 @@
     partner = chip * 2 + other
     right_chip, left_chip = lax.rem(chip + 1, chips), lax.rem(chip + chips - 1, chips)
     far_chip = lax.rem(chip + 2, chips)
-    right, left = right_chip * 2 + core, left_chip * 2 + core
+    right, left, far = right_chip * 2 + core, left_chip * 2 + core, far_chip * 2 + core
 
     def remote(src, dst, send_sem, recv_sem, device):
         return pltpu.make_async_remote_copy(src_ref=src, dst_ref=dst, send_sem=send_sem, recv_sem=recv_sem,
@@ -49,8 +52,9 @@
 
     pair_cols = 2 * width
     n_q = q_cols // pair_cols
-    n_o = 4
-    o_depth = wo_hbm.shape[1] // n_o
+    o_depth = d_model
+    n_o = wo_hbm.shape[1] // o_depth
+    wo_base = wa.shape[1] - n_o * half_d
     kv_parts = rows // GROUP
 
     def q_copy(l, p):
@@ -61,12 +65,16 @@
     def o_copy(l, p):
         col = pl.multiple_of(core * half_d, LANES)
         return pltpu.make_async_copy(wo_hbm.at[l, p * o_depth:(p + 1) * o_depth, pl.ds(col, half_d)],
-                                     wb.at[p * o_depth:(p + 1) * o_depth, :], w_sem.at[n_q + p])
+                                     wa.at[:, wo_base + p * half_d:wo_base + (p + 1) * half_d], w_sem.at[n_q + p])
 
     def ffn_copies(l):
         return [pltpu.make_async_copy(wg_hbm.at[l], wa.at[:, 0:ffn], w_sem.at[n_q + n_o]),
                 pltpu.make_async_copy(wu_hbm.at[l], wa.at[:, ffn:2 * ffn], w_sem.at[n_q + n_o + 1]),
                 pltpu.make_async_copy(wd_hbm.at[l], wa.at[0:ffn, 2 * ffn:2 * ffn + d_model], w_sem.at[n_q + n_o + 2])]
+
+    def head_copy(which):
+        cols = (slice(wo_base, wa.shape[1]), slice(0, wo_base))[which]
+        return pltpu.make_async_copy(w_head_hbm.at[:, cols], wa.at[:, cols], head_sem.at[which])
 
     def kv_copy(l, g):
         return pltpu.make_async_copy(kv_hbm.at[l, g * GROUP:(g + 1) * GROUP],
@@ -80,9 +88,9 @@
         o_copy(0, p).start()
 
     barrier = pltpu.get_barrier_semaphore()
-    for device in (partner, left, right):
+    for device in (partner, left, right, far):
         pl.semaphore_signal(barrier, inc=1, device_id={"dp": device}, device_id_type=MESH)
-    pl.semaphore_wait(barrier, 3)
+    pl.semaphore_wait(barrier, 4)
 
     if width % LANES:
         q_s[q_parts - 1] = jnp.zeros(q_s.shape[1:], F32)
@@ -96,57 +104,76 @@
     def half_cols(which, t=0, n=None):
         return pl.ds(pl.multiple_of(which * half_d + t * TILE, LANES), half_d if n is None else n)
 
-    def gather_rows(gain_row, dst):
-        def piece(which_chip, half, count=rows):
-            return xg.at[pl.ds(pl.multiple_of(which_chip * pair + half * rows, rows), count), half_cols(core)]
-
-        def send(which_chip, half, slot, device):
-            copy = remote(piece(which_chip, half), piece(which_chip, half), ag_send.at[slot], ag_recv.at[slot], device)
-            copy.start()
-            return copy
-
-        def pass_on(which_chip, half, slot, count=rows):
-            copy = remote(piece(which_chip, half, count), piece(which_chip, half, count),
-                          d2d_send.at[slot], d2d_recv.at[slot], partner)
-            copy.start()
-            return copy
-
-        def norm(which_chip):
+    def rows_of(which_chip, half, count=rows):
+        return pl.ds(pl.multiple_of(which_chip * pair + half * rows, rows), count)
+
+    ring_pieces = ((chip, 0, right), (chip, 1, left), (chip, 1, right), (chip, 0, left), (left_chip, 0, right), (right_chip, 1, left),
+                   (chip, 0, far), (chip, 1, far))
+    pair_pieces = ((chip, 0), (left_chip, 0), (right_chip, 1), (left_chip, 1), (right_chip, 0), (far_chip, 0), (far_chip, 1))
+
+    def ring_copy(slot, t):
+        which_chip, half, device = ring_pieces[slot]
+        at = xg.at[rows_of(which_chip, half), half_cols(core, t, TILE)]
+        slot = slot - 2 if slot >= 6 else slot
+        return remote(at, at, ag_send.at[slot, t], ag_recv.at[slot, t], device)
+
+    def pair_copy(slot, t):
+        which_chip, half = pair_pieces[slot]
+        at = xg.at[rows_of(which_chip, half, rows if slot else pair), half_cols(core, t, TILE)]
+        return remote(at, at, d2d_send.at[slot, t], d2d_recv.at[slot, t], partner)
+
+    def gather_start(t):
+        def straight():
+            ring_copy(6, t).start()
+            ring_copy(7, t).start()
+
+        if isinstance(t, int):
+            if t >= AG_STRAIGHT:
+                straight()
+        else:
+            pl.when(t >= AG_STRAIGHT)(straight)
+        for slot in range(4):
+            ring_copy(slot, t).start()
+        pair_copy(0, t).start()
+
+    def gather_near(t):
+        for slot in range(4):
+            ring_copy(slot, t).wait_recv()
+            if slot < 2 and t < AG_STRAIGHT:
+                ring_copy(4 + slot, t).start()
+            pair_copy(1 + slot, t).start()
+
+    def gather_end(first, gain_row, dst):
+        def arrived(slots, which_chip):
+            for slot in slots:
+                for t in range(t_tiles):
+                    pair_copy(slot, t).wait_recv()
             at = pl.ds(pl.multiple_of(which_chip * pair, pair), pair)
             dst[at, :] = rms_norm(xg[at, :].astype(F32), gain_row)
 
-        own_a = send(chip, 0, 0, right)
-        own_b = send(chip, 1, 1, left)
-        own_b2 = send(chip, 1, 2, right)
-        own_a2 = send(chip, 0, 3, left)
-        passed = [pass_on(chip, 0, 0, pair)]
-        own_a.wait_recv()
-        far_a = send(left_chip, 0, 4, right)
-        own_b.wait_recv()
-        far_b = send(right_chip, 1, 5, left)
-        passed.append(pass_on(left_chip, 0, 1))
-        passed.append(pass_on(right_chip, 1, 2))
-        passed[0].wait_recv()
-        norm(chip)
-        own_b2.wait_recv()
-        passed.append(pass_on(left_chip, 1, 3))
-        own_a2.wait_recv()
-        passed.append(pass_on(right_chip, 0, 4))
-        passed[1].wait_recv()
-        passed[3].wait_recv()
-        norm(left_chip)
-        passed[2].wait_recv()
-        passed[4].wait_recv()
-        norm(right_chip)
-        far_a.wait_recv()
-        passed.append(pass_on(far_chip, 0, 5))
-        far_b.wait_recv()
-        passed.append(pass_on(far_chip, 1, 6))
-        passed[5].wait_recv()
-        passed[6].wait_recv()
-        norm(far_chip)
-        for copy in [own_a, own_b, own_b2, own_a2, far_a, far_b] + passed:
-            copy.wait_send()
+        def gather_far(t):
+            for slot in range(2):
+                ring_copy(4 + slot, t).wait_recv()
+                pair_copy(5 + slot, t).start()
+
+        for t in range(first, t_tiles - 1):
+            gather_near(t)
+        arrived((0,), chip)
+        gather_near(t_tiles - 1)
+        for t in range(AG_STRAIGHT):
+            gather_far(t)
+        arrived((1, 3), left_chip)
+        arrived((2, 4), right_chip)
+        for t in range(AG_STRAIGHT, t_tiles):
+            gather_far(t)
+        arrived((5, 6), far_chip)
+        for t in range(t_tiles):
+            for slot in range(4):
+                ring_copy(slot, t).wait_send()
+            for slot in range(2):
+                ring_copy((6 if t >= AG_STRAIGHT else 4) + slot, t).wait_send()
+            for slot in range(7):
+                pair_copy(slot, t).wait_send()
 
     own_chip_rows = pl.ds(pl.multiple_of(chip * pair, pair), pair)
 
@@ -175,7 +202,7 @@
 
         o_copies = []
         per_half = kv_parts // 2
-        key_pos = lax.broadcasted_iota(jnp.int32, (heads, kv_b.shape[1]), 1)
+        key_pos = lax.broadcasted_iota(jnp.int32, (heads, kv_b.shape[2]), 1)
         for half in range(2):
             for g in range(half * per_half, (half + 1) * per_half):
                 kv_copy(layer, g).wait()
@@ -184,14 +211,15 @@
                     b = g * GROUP + i
                     at = pl.ds(core * rows + b, heads, stride=pair)
                     q_b = jnp.concatenate([q_s[c, at, :] for c in range(q_parts)], axis=1)[:, 0:width].astype(BF16)
-                    s_b = lax.dot_general(q_b, kv_b[b], (((1,), (1,)), ((), ())), preferred_element_type=F32) * QK_SCALE
+                    s_b = jnp.dot(q_b, kv_b[b], preferred_element_type=F32) * QK_SCALE
                     scores.append(jnp.where(key_pos < lengths[b], s_b, -1e30))
                 s_all = jnp.concatenate(scores, axis=0)
                 e_all = jnp.exp(s_all - jnp.max(s_all, axis=-1, keepdims=True))
                 p_all = (e_all / jnp.sum(e_all, axis=-1, keepdims=True)).astype(BF16)
                 for i in range(GROUP):
                     b = g * GROUP + i
-                    o_b = jnp.dot(p_all[i * heads:(i + 1) * heads, :], kv_b[b, :, 0:LATENT_DIM], preferred_element_type=F32)
+                    o_b = lax.dot_general(p_all[i * heads:(i + 1) * heads, :], kv_b[b, 0:LATENT_DIM, :],
+                                          (((1,), (1,)), ((), ())), preferred_element_type=F32)
                     for c in range(LATENT_DIM // LANES):
                         o_s[c, pl.ds(b, heads, stride=rows), :] = o_b[:, c * LANES:(c + 1) * LANES]
                 if layer + 1 < num_layers:
@@ -214,10 +242,13 @@
             copy.wait_recv()
 
         def wo_tile(t, carry):
-            cols = pl.ds(pl.multiple_of(t * TILE, TILE), TILE)
-            o_val = jnp.dot(o_all[...], wb[:, cols], preferred_element_type=F32)
+            o_val = jnp.zeros((pair, TILE), F32)
+            for p in range(n_o):
+                cols = pl.ds(pl.multiple_of(wo_base + p * half_d + t * TILE, LANES), TILE)
+                o_val += jnp.dot(o_all[:, p * o_depth:(p + 1) * o_depth], wa[:, cols], preferred_element_type=F32)
             xg[own_chip_rows, half_cols(core, t, TILE)] = \
                 (x_full[:, half_cols(core, t, TILE)].astype(F32) + o_val).astype(BF16)
+            gather_start(t)
             return carry
 
         lax.fori_loop(0, t_tiles, wo_tile, 0)
@@ -226,34 +257,28 @@
         if layer + 1 < num_layers:
             for p in range(n_o):
                 o_copy(layer + 1, p).start()
-
-        gather_rows(norm_ffn[layer:layer + 1, :], out)
+        else:
+            head_copy(0).start()
+
+        gather_end(0, norm_ffn[layer:layer + 1, :], out)
         for copy in ffn_copies(layer):
             copy.wait()
 
-        def gate_up(j, carry):
-            at = pl.ds(pl.multiple_of(j * LANES, LANES), LANES)
-            at_up = pl.ds(pl.multiple_of(ffn + j * LANES, LANES), LANES)
-            both = jnp.concatenate([wa[:, at], wa[:, at_up]], axis=1)
+        for j in range(0, ffn, LANES):
+            both = jnp.concatenate([wa[:, j:j + LANES], wa[:, ffn + j:ffn + j + LANES]], axis=1)
             val = jnp.dot(out[...], both, preferred_element_type=F32)
-            act[:, at] = (jax.nn.silu(val[:, :LANES]) * val[:, LANES:]).astype(BF16)
-            return carry
-
-        lax.fori_loop(0, ffn // LANES, gate_up, 0)
+            act[:, j:j + LANES] = (jax.nn.silu(val[:, :LANES]) * val[:, LANES:]).astype(BF16)
 
         def down(which, t):
             cols = pl.ds(pl.multiple_of(2 * ffn + which * half_d + t * TILE, LANES), TILE)
             return jnp.dot(act[...], wa[0:ffn, cols], preferred_element_type=F32)
 
         y_copies = []
-        for t in range(t_tiles):
+        def away(t):
             y_send[t] = down(other, t)
             copy = remote(y_send.at[t], y_recv.at[t], y_ssem.at[t], y_rsem.at[t], partner)
             copy.start()
             y_copies.append(copy)
-
-        def rows_of(which_chip, half):
-            return pl.ds(pl.multiple_of(which_chip * pair + half * rows, rows), rows)
 
         def rs_copy(src, dst, slot, t, device):
             copy = remote(src, dst, rs_send.at[slot, t], rs_recv.at[slot, t], device)
@@ -268,21 +293,30 @@
                 relay_out[d, t] = relay_in[d, t] + y_sum[t, rows_of(target, d), :]
                 rs_final[t].append(rs_copy(relay_out.at[d, t], direct_in.at[2 + d, t], 4 + d, t, device))
 
-        for t in range(t_tiles):
-            own = down(core, t)
+        def own(t):
+            val = down(core, t)
             y_copies[t].wait_recv()
-            y_sum[t] = own + y_recv[t]
+            y_sum[t] = val + y_recv[t]
             rs_relay.append([rs_copy(y_sum.at[t, rows_of(far_chip, 0), :], relay_in.at[0, t], 0, t, right),
                              rs_copy(y_sum.at[t, rows_of(far_chip, 1), :], relay_in.at[1, t], 1, t, left)])
             rs_direct.append([rs_copy(y_sum.at[t, rows_of(right_chip, 1), :], direct_in.at[0, t], 2, t, right),
                               rs_copy(y_sum.at[t, rows_of(left_chip, 0), :], direct_in.at[1, t], 3, t, left)])
             rs_final.append([])
-            if t >= 1:
-                relay(t - 1)
-        relay(t_tiles - 1)
+
+        away(0)
+        for t in range(t_tiles):
+            if t + 1 < t_tiles:
+                away(t + 1)
+            own(t)
+            if t >= RS_LAG:
+                relay(t - RS_LAG)
+        for t in range(t_tiles - RS_LAG, t_tiles):
+            relay(t)
         if layer + 1 < num_layers:
             for p in range(n_q):
                 q_copy(layer + 1, p).start()
+        else:
+            head_copy(1).start()
 
         last = layer + 1 == num_layers
         x_copies = []
@@ -297,7 +331,11 @@
                     xg[rows_of(chip, half), cols] = x_new
                 else:
                     x_full[half * rows:(half + 1) * rows, cols] = x_new
-            if not last:
+            if last:
+                gather_start(t)
+                if t >= AG_LAG:
+                    gather_near(t - AG_LAG)
+            else:
                 copy = remote(x_full.at[:, cols], x_full.at[:, cols], x_send.at[1 + t], x_recv.at[1 + t], partner)
                 copy.start()
                 x_copies.append(copy)
@@ -309,10 +347,96 @@
         for copy in x_copies:
             copy.wait()
 
-    gather_rows(norm_final[0:1, :], out)
-
-
-def decode_layers(n_dev, lengths, hidden, kv_cache, norm_attn, w_q, w_o, norm_ffn, w_gate, w_up, w_down, norm_final):
+    gather_end(t_tiles - AG_LAG, norm_final[0:1, :], out)
+    head_copy(0).wait()
+    head_copy(1).wait()
+
+
+def head_kernel(h_ref, ahead, w_hbm, out_hbm, ring, stage, w_sem, out_sem):
+    slots, _, tile = ring.shape
+    n_stage = stage.shape[0]
+    n_ahead = ahead.shape[1] // tile
+    n_stream = w_hbm.shape[1] // tile - n_ahead
+
+    def col(t):
+        return pl.ds(pl.multiple_of(t * tile, tile), tile)
+
+    def fetch(i, slot):
+        return pltpu.make_async_copy(w_hbm.at[:, col(n_ahead + i)], ring.at[slot], w_sem.at[slot])
+
+    def put(t, slot):
+        return pltpu.make_async_copy(stage.at[slot], out_hbm.at[:, col(t)], out_sem.at[slot])
+
+    for i in range(slots):
+        fetch(i, i).start()
+
+    def tiles(n, jobs):
+        for e, _ in enumerate(jobs):
+            @pl.when(n + e >= n_stage)
+            def _():
+                put(0, lax.rem(n + e, n_stage)).wait()
+        for e, (t, weights) in enumerate(jobs):
+            for c in range(0, tile, TILE):
+                stage[lax.rem(n + e, n_stage), :, c:c + TILE] = \
+                    jnp.dot(h_ref[...], weights(c), preferred_element_type=F32)
+        for e, (t, weights) in enumerate(jobs):
+            put(t, lax.rem(n + e, n_stage)).start()
+
+    def from_ahead(i):
+        return i, lambda c: ahead[:, pl.ds(pl.multiple_of(i * tile + c, TILE), TILE)]
+
+    def from_ring(i):
+        return n_ahead + i, lambda c: ring[lax.rem(i, slots), :, c:c + TILE]
+
+    def refill(i):
+        @pl.when(i + slots < n_stream)
+        def _():
+            fetch(i + slots, lax.rem(i, slots)).start()
+
+    n_both = n_ahead - 2
+
+    def both(i, carry):
+        fetch(i, lax.rem(i, slots)).wait()
+        tiles(2 * i + 2, [from_ahead(i + 2), from_ring(i)])
+        refill(i)
+        return carry
+
+    def alone(j, carry):
+        i = n_both + 2 * j
+        for e in range(2):
+            fetch(i + e, lax.rem(i + e, slots)).wait()
+        tiles(n_ahead + i, [from_ring(i), from_ring(i + 1)])
+        for e in range(2):
+            refill(i + e)
+        return carry
+
+    tiles(0, [from_ahead(0), from_ahead(1)])
+    lax.fori_loop(0, n_both, both, 0)
+    lax.fori_loop(0, (n_stream - n_both) // 2, alone, 0)
+    for s in range(n_stage):
+        put(0, s).wait()
+
+
+def head_matmul(gathered, ahead, w_head):
+    tile, slots, n_stage = 1024, 3, 4
+    depth, cols = w_head.shape
+    rows = gathered.shape[0]
+    hbm, vmem = pl.BlockSpec(memory_space=pl.ANY), pl.BlockSpec(memory_space=pltpu.VMEM)
+    return pl.pallas_call(
+        head_kernel,
+        out_shape=jax.ShapeDtypeStruct((rows, cols), F32),
+        in_specs=[vmem, vmem, hbm],
+        out_specs=hbm,
+        scratch_shapes=[pltpu.VMEM((slots, depth, tile), BF16), pltpu.VMEM((n_stage, rows, tile), F32),
+                        pltpu.SemaphoreType.DMA((slots,)), pltpu.SemaphoreType.DMA((n_stage,))],
+        compiler_params=pltpu.CompilerParams(vmem_limit_bytes=22 * 1024 * 1024),
+        cost_estimate=pl.CostEstimate(flops=2 * rows * depth * cols, bytes_accessed=2 * depth * cols + 4 * rows * cols,
+                                      transcendentals=0),
+        name="head_matmul",
+    )(gathered, ahead, w_head)
+
+
+def decode_layers(n_dev, lengths, hidden, kv_cache, norm_attn, w_q, w_o, norm_ffn, w_gate, w_up, w_down, norm_final, w_head):
     num_layers, rows, seq_len, width = kv_cache.shape
     d_model = hidden.shape[1]
     heads = w_q.shape[2] // width
@@ -329,9 +453,7 @@
     cfg = (num_layers, rows, heads, width, d_model, ffn, n_dev)
     n_q = q_cols // (2 * width)
     scratch = [
-        pltpu.VMEM((d_model, wa_cols), BF16),
-        pltpu.VMEM((w_o.shape[1], half_d), BF16),
-        pltpu.VMEM((rows, seq_len, width), BF16),
+        pltpu.VMEM((rows, width, seq_len), BF16),
         pltpu.VMEM((pair, d_model), BF16),
         pltpu.VMEM((pair, d_model), BF16),
         pltpu.VMEM((pad_width // LANES, heads * pair, LANES), F32),
@@ -347,23 +469,26 @@
         pltpu.VMEM((4, t_tiles, rows, TILE), F32),
         dma((n_q + 4 + 3,)),
         dma((rows // GROUP,)),
+        dma((2,)),
         dma((1 + t_tiles,)), dma((1 + t_tiles,)),
         dma((2 * n_q,)), dma((2 * n_q,)),
         dma((2,)), dma((2,)),
-        dma((6,)), dma((6,)),
-        dma((7,)), dma((7,)),
+        dma((6, t_tiles)), dma((6, t_tiles)),
+        dma((7, t_tiles)), dma((7, t_tiles)),
         dma((t_tiles,)), dma((t_tiles,)),
         dma((6, t_tiles)), dma((6, t_tiles)),
     ]
-    return pl.pallas_call(
+    gathered, ahead = pl.pallas_call(
         functools.partial(decode_kernel, cfg),
-        out_shape=jax.ShapeDtypeStruct((group_rows, d_model), BF16),
-        in_specs=[smem, vmem, hbm, vmem, hbm, hbm, vmem, hbm, hbm, hbm, vmem],
-        out_specs=vmem,
+        out_shape=(pltpu.VMEM((group_rows, d_model), BF16), pltpu.VMEM((d_model, wa_cols + w_o.shape[1] // d_model * half_d), BF16)),
+        in_specs=[smem, vmem, hbm, vmem, hbm, hbm, vmem, hbm, hbm, hbm, vmem, hbm],
+        out_specs=(vmem, vmem),
         scratch_shapes=scratch,
-        compiler_params=pltpu.CompilerParams(collective_id=0, has_side_effects=True, vmem_limit_bytes=64 * 1000 * 1000),
+        compiler_params=pltpu.CompilerParams(collective_id=0, has_side_effects=True, vmem_limit_bytes=26 * 1024 * 1024),
         name="decode_layers",
-    )(lengths, hidden, kv_cache, norm_attn, w_q, w_o, norm_ffn, w_gate, w_up, w_down, norm_final.reshape(1, -1))
+    )(lengths, hidden, jnp.swapaxes(kv_cache, 2, 3), norm_attn, w_q, w_o, norm_ffn, w_gate, w_up, w_down, norm_final.reshape(1, -1), w_head)
+    gathered, ahead = (pltpu.with_memory_space_constraint(a, pltpu.VMEM) for a in (gathered, ahead))
+    return head_matmul(gathered, ahead, w_head)
 
 
 def solution(mesh):
@@ -373,8 +498,7 @@
     n_dev = mesh.shape['dp']
 
     def device_step(hidden, lengths, kv_cache, norm_attn, w_q, w_o, norm_ffn, w_gate, w_up, w_down, norm_final, w_head):
-        gathered = decode_layers(n_dev, lengths, hidden, kv_cache, norm_attn, w_q, w_o, norm_ffn, w_gate, w_up, w_down,
-                                 norm_final)
-        return jnp.dot(gathered, w_head, preferred_element_type=jnp.float32)
+        return decode_layers(n_dev, lengths, hidden, kv_cache, norm_attn, w_q, w_o, norm_ffn, w_gate, w_up, w_down,
+                             norm_final, w_head)
 
     return jax.shard_map(device_step, mesh=mesh, in_specs=specs_in, out_specs=P('rep', 'dp'), check_vma=False)

time: 160 us -> 125 us (0.78)
  matrix products: 38 us -> 0 us
  Pallas kernels: 108 us -> 125 us
  local copies, waits for them, and re-layouts: 13.6 us -> 0 us
    dot_general x1 -> x0, matrix products: 38 us -> none  [device_step(): return jnp.dot(gathered, w_head, preferred_element_type=jnp.float32)]
    pallas_call x1 -> x2, Pallas kernels: 108 us -> 125 us  [the longest x1 93.8 us: decode_layers(): pl.pallas_call(functools.partial(decode_kernel, cfg), out_shape=(pltpu.VM...]
    unnamed x1 -> x0, local copies, waits for them, and re-layouts: 13.6 us -> none
where the time goes in v2:
time: 125 us
  Pallas kernels  125 us (100%)
    pallas_call x1, Pallas kernels, decode_layers(): pl.pallas_call(functools.partial(decode_kernel, cfg), out_shape=(pltpu.VM...  93.8 us
    pallas_call x1, Pallas kernels, head_matmul(): pl.pallas_call(head_kernel, out_shape=jax.ShapeDtypeStruct((rows, cols),...  31.3 us

profile of v2, /device:TPU:113, one launch (start us, length us, event | category | flops | bytes accessed | tf_op | source)
XLA Modules:
  0.0 125.2 jit_solution(8006948886140755775)
XLA Ops:
  0.0 93.8 %decode_layers.1 = (bf16[256,2048]{1,0:T(8,128)(2,1)S(1)}, bf16[2048,8960]{1,0:T(8,128)(2,1)S(1)}) custom-call(s32[32]{0:T(128)} %lengths.1, bf16[32,2048]{1,0:T(8,128)(2,1)} %hidden.1, bf16[2,32,576,128]{3,2,1,0:T(8,128)(2,1)} %bitcast.2, f32[2,2048]{1,0:T(2,128)} %norm_attn.1, bf16[2,2048,9216]{2,1,0:T(8,128)(2,1)} %wq_hbm.1, ...), custom_call_target="tpu_custom_call" | custom-call | tf_op jit(solution)/shard_map/decode_layers/pallas_call | solution.py:481
  93.8 31.3 %head_matmul.1 = f32[256,20480]{1,0:T(8,128)} custom-call(bf16[256,2048]{1,0:T(8,128)(2,1)S(1)} %get-tuple-element.7.h_ref, bf16[2048,8960]{1,0:T(8,128)(2,1)S(1)} %get-tuple-element.8.ahead, bf16[2048,20480]{1,0:T(8,128)(2,1)} %w_hbm.1), custom_call_target="tpu_custom_call" | custom-call | flops 21474836480 | bytes 104857600 | tf_op jit(solution)/shard_map/head_matmul/pallas_call | solution.py:425

commit v3 on v2

--- a/solution.py
+++ b/solution.py
@@ -354,12 +354,15 @@
 
 def head_kernel(h_ref, ahead, w_hbm, out_hbm, ring, stage, w_sem, out_sem):
     slots, _, tile = ring.shape
-    n_stage = stage.shape[0]
+    per_s, per_a = slots // 2, 2
+    per = per_s + per_a
     n_ahead = ahead.shape[1] // tile
     n_stream = w_hbm.shape[1] // tile - n_ahead
-
-    def col(t):
-        return pl.ds(pl.multiple_of(t * tile, tile), tile)
+    n_steps = n_stream // per_s
+    n_before, n_after = n_ahead - per_a * n_steps, n_stream - per_s * n_steps
+
+    def col(t, c=0, n=tile):
+        return pl.ds(pl.multiple_of(t * tile + c, TILE), n)
 
     def fetch(i, slot):
         return pltpu.make_async_copy(w_hbm.at[:, col(n_ahead + i)], ring.at[slot], w_sem.at[slot])
@@ -367,58 +370,55 @@
     def put(t, slot):
         return pltpu.make_async_copy(stage.at[slot], out_hbm.at[:, col(t)], out_sem.at[slot])
 
-    for i in range(slots):
-        fetch(i, i).start()
-
-    def tiles(n, jobs):
-        for e, _ in enumerate(jobs):
-            @pl.when(n + e >= n_stage)
+    def tiles(jobs):
+        for t, weights, slot in jobs:
+            for c in range(0, tile, TILE):
+                stage[slot, :, c:c + TILE] = jnp.dot(h_ref[...], weights(c), preferred_element_type=F32)
+        for t, weights, slot in jobs:
+            put(t, slot).start()
+
+    def from_ahead(i, slot):
+        return i, lambda c: ahead[:, col(i, c, TILE)], slot
+
+    def from_ring(i, ring_slot, slot):
+        return n_ahead + i, lambda c: ring[ring_slot, :, c:c + TILE], slot
+
+    for e in range(per_s):
+        fetch(e, e).start()
+    tiles([from_ahead(e, 2 * per + e) for e in range(n_before)])
+    for e in range(per_s, slots):
+        fetch(e, e).start()
+
+    def step(i, carry):
+        side = lax.rem(i, 2)
+        for e in range(per_s):
+            fetch(i * per_s + e, side * per_s + e).wait()
+
+        @pl.when(i >= 2)
+        def _():
+            for e in range(per):
+                put(0, side * per + e).wait()
+        tiles([from_ring(i * per_s + e, side * per_s + e, side * per + e) for e in range(per_s)])
+        for e in range(per_s):
+            @pl.when(i * per_s + e + slots < n_stream)
             def _():
-                put(0, lax.rem(n + e, n_stage)).wait()
-        for e, (t, weights) in enumerate(jobs):
-            for c in range(0, tile, TILE):
-                stage[lax.rem(n + e, n_stage), :, c:c + TILE] = \
-                    jnp.dot(h_ref[...], weights(c), preferred_element_type=F32)
-        for e, (t, weights) in enumerate(jobs):
-            put(t, lax.rem(n + e, n_stage)).start()
-
-    def from_ahead(i):
-        return i, lambda c: ahead[:, pl.ds(pl.multiple_of(i * tile + c, TILE), TILE)]
-
-    def from_ring(i):
-        return n_ahead + i, lambda c: ring[lax.rem(i, slots), :, c:c + TILE]
-
-    def refill(i):
-        @pl.when(i + slots < n_stream)
-        def _():
-            fetch(i + slots, lax.rem(i, slots)).start()
-
-    n_both = n_ahead - 2
-
-    def both(i, carry):
-        fetch(i, lax.rem(i, slots)).wait()
-        tiles(2 * i + 2, [from_ahead(i + 2), from_ring(i)])
-        refill(i)
+                fetch(i * per_s + e + slots, side * per_s + e).start()
+        tiles([from_ahead(n_before + i * per_a + e, side * per + per_s + e) for e in range(per_a)])
         return carry
 
-    def alone(j, carry):
-        i = n_both + 2 * j
-        for e in range(2):
-            fetch(i + e, lax.rem(i + e, slots)).wait()
-        tiles(n_ahead + i, [from_ring(i), from_ring(i + 1)])
-        for e in range(2):
-            refill(i + e)
-        return carry
-
-    tiles(0, [from_ahead(0), from_ahead(1)])
-    lax.fori_loop(0, n_both, both, 0)
-    lax.fori_loop(0, (n_stream - n_both) // 2, alone, 0)
-    for s in range(n_stage):
-        put(0, s).wait()
+    lax.fori_loop(0, n_steps, step, 0)
+    last = n_steps * per_s
+    for e in range(n_after):
+        fetch(last + e, (last + e) % slots).wait()
+    for e in range(n_before):
+        put(0, 2 * per + e).wait()
+    tiles([from_ring(last + e, (last + e) % slots, 2 * per + e) for e in range(n_after)])
+    for slot in range(2 * per + n_after):
+        put(0, slot).wait()
 
 
 def head_matmul(gathered, ahead, w_head):
-    tile, slots, n_stage = 1024, 3, 4
+    tile, slots, n_stage = 512, 6, 13
     depth, cols = w_head.shape
     rows = gathered.shape[0]
     hbm, vmem = pl.BlockSpec(memory_space=pl.ANY), pl.BlockSpec(memory_space=pltpu.VMEM)

time: 125 us -> 121 us (0.968)
  Pallas kernels: 125 us -> 120 us
    pallas_call x1, Pallas kernels: 31.3 us -> 26.5 us  [head_matmul(): pl.pallas_call(head_kernel, out_shape=jax.ShapeDtypeStruct((rows, cols),...]
where the time goes in v3:
time: 121 us; the launch traced here: 120 us
  Pallas kernels  120 us (99%)
    pallas_call x1, Pallas kernels, decode_layers(): pl.pallas_call(functools.partial(decode_kernel, cfg), out_shape=(pltpu.VM...  93.8 us
    pallas_call x1, Pallas kernels, head_matmul(): pl.pallas_call(head_kernel, out_shape=jax.ShapeDtypeStruct((rows, cols),...  26.5 us

profile of v3, /device:TPU:113, one launch (start us, length us, event | category | flops | bytes accessed | tf_op | source)
XLA Modules:
  0.0 120.5 jit_solution(11739453365524841891)
XLA Ops:
  0.0 93.8 %decode_layers.1 = (bf16[256,2048]{1,0:T(8,128)(2,1)S(1)}, bf16[2048,8960]{1,0:T(8,128)(2,1)S(1)}) custom-call(s32[32]{0:T(128)} %lengths.1, bf16[32,2048]{1,0:T(8,128)(2,1)} %hidden.1, bf16[2,32,576,128]{3,2,1,0:T(8,128)(2,1)} %bitcast.2, f32[2,2048]{1,0:T(2,128)} %norm_attn.1, bf16[2,2048,9216]{2,1,0:T(8,128)(2,1)} %wq_hbm.1, ...), custom_call_target="tpu_custom_call" | custom-call | tf_op jit(solution)/shard_map/decode_layers/pallas_call | solution.py:481
  93.8 26.5 %head_matmul.1 = f32[256,20480]{1,0:T(8,128)} custom-call(bf16[256,2048]{1,0:T(8,128)(2,1)S(1)} %get-tuple-element.7.h_ref, bf16[2048,8960]{1,0:T(8,128)(2,1)S(1)} %get-tuple-element.8.ahead, bf16[2048,20480]{1,0:T(8,128)(2,1)} %w_hbm.1), custom_call_target="tpu_custom_call" | custom-call | flops 21474836480 | bytes 104857600 | tf_op jit(solution)/shard_map/head_matmul/pallas_call | solution.py:425
